TPU v7x, 256 devices: a whole 4x4x8 slice. The times are simulated.
256 devices in a mesh: row: 8 (over x, y_hi), col: 32 (over z, y_lo, core).
Axes of the slice: x: 4, y: 4 (y_hi: 2, y_lo: 2; y = y_hi * 2 + y_lo), z: 8, core: 2. Of those that a mesh axis runs over, the one named last changes fastest.
Arguments:
- e_field: float32 [3, 64, 64, 4096], P(None, None, 'row', 'col'), may hold values from -6 to 6
- h_field: float32 [3, 64, 64, 4096], P(None, None, 'row', 'col'), may hold values from -6 to 6
- e_coef: float32 [64, 64, 4096], P(None, 'row', 'col'), may hold values from 0.125 to 0.5
- basis: float32 [128, 64, 4096], P('row', None, 'col'), may hold values from -0.01171875 to 0.01171875
- pml_width: int32 [4], replicated, may hold values from 2 to 8
- snap_index: int32 [64], replicated, may hold values from 0 to 383
Outputs:
- e_final: float32 [3, 64, 64, 4096], P(None, None, 'row', 'col')
- h_final: float32 [3, 64, 64, 4096], P(None, None, 'row', 'col')
- coefficients: float32 [64, 128], replicated
- gram: float32 [64, 64], replicated
All inputs are finite; a program needn't handle non-finite values.
Results may differ from a plain program's by a relative error of at most 0.00008.
Values sent between devices are 32-bit elements; how exact they have to be, the bound alone decides.
No kernel may reach another device: no remote copies, remote signals or barrier semaphores. Data moves between devices by JAX's collectives and lax.ppermute only.
A program may use at most 64 MiB of HBM per device.

v0:
```python
import jax
import jax.numpy as jnp
from jax import lax
from jax.sharding import Mesh
from jax.sharding import PartitionSpec as P

STEPS = 8
ROW = ("row_0", "row_1")
COL = ("col_0", "col_1", "col_2")
ROW_COL = ("row_0", "row_1", "col_0", "col_1", "col_2")
time_step = 0.5
sigma_top = 4.0
alpha_shift = 0.05


def from_behind(block, axis, distance):
    devices = range(lax.axis_size(axis))
    route = [(i - distance, i) for i in devices if i - distance in devices]
    return lax.ppermute(block, axis, route)


def by_axis(array, axes):
    for axis in axes:
        array = lax.psum(array, axis)
    return array


def forward(field, axis, plane):
    count = field.shape[axis]
    after = jnp.concatenate(
        [lax.slice_in_dim(field, 1, count, axis=axis), jnp.expand_dims(plane, axis)], axis
    )
    return after - field


def backward(field, axis, plane):
    count = field.shape[axis]
    before = jnp.concatenate(
        [jnp.expand_dims(plane, axis), lax.slice_in_dim(field, 0, count - 1, axis=axis)], axis
    )
    return field - before


def absorber(positions, total, low, high):
    depth = jnp.maximum(
        jnp.maximum((low - positions) / low, (positions - (total - 1.0 - high)) / high), 0.0
    )
    sigma = sigma_top * depth**3
    damp = jnp.exp(-(sigma + alpha_shift) * time_step)
    gain = sigma / (sigma + alpha_shift) * (damp - 1.0)
    return (damp, gain)


def magnetic(e_field, h_field, psi, next_x, next_y, damp_x, gain_x, damp_y, gain_y):
    e_x, e_y, e_z = (e_field[0], e_field[1], e_field[2])
    h_x, h_y, h_z = (h_field[0], h_field[1], h_field[2])
    zplane = jnp.zeros_like(e_x[0])
    ez_dy = forward(e_z, 2, next_y[1])
    ey_dz = forward(e_y, 0, zplane)
    ex_dz = forward(e_x, 0, zplane)
    ez_dx = forward(e_z, 1, next_x[1])
    ey_dx = forward(e_y, 1, next_x[0])
    ex_dy = forward(e_x, 2, next_y[0])
    psi_hxy = damp_y * psi[0] + gain_y * ez_dy
    psi_hyx = damp_x * psi[1] + gain_x * ez_dx
    psi_hzx = damp_x * psi[2] + gain_x * ey_dx
    psi_hzy = damp_y * psi[3] + gain_y * ex_dy
    h_x = h_x - time_step * (ez_dy + psi_hxy - ey_dz)
    h_y = h_y - time_step * (ex_dz - ez_dx - psi_hyx)
    h_z = h_z - time_step * (ey_dx + psi_hzx - ex_dy - psi_hzy)
    return (jnp.stack((h_x, h_y, h_z)), (psi_hxy, psi_hyx, psi_hzx, psi_hzy))


def electric(e_field, h_field, psi, e_coef, prev_x, prev_y, damp_x, gain_x, damp_y, gain_y):
    e_x, e_y, e_z = (e_field[0], e_field[1], e_field[2])
    h_x, h_y, h_z = (h_field[0], h_field[1], h_field[2])
    zplane = jnp.zeros_like(h_x[0])
    hz_dy = backward(h_z, 2, prev_y[1])
    hy_dz = backward(h_y, 0, zplane)
    hx_dz = backward(h_x, 0, zplane)
    hz_dx = backward(h_z, 1, prev_x[1])
    hy_dx = backward(h_y, 1, prev_x[0])
    hx_dy = backward(h_x, 2, prev_y[0])
    psi_exy = damp_y * psi[0] + gain_y * hz_dy
    psi_eyx = damp_x * psi[1] + gain_x * hz_dx
    psi_ezx = damp_x * psi[2] + gain_x * hy_dx
    psi_ezy = damp_y * psi[3] + gain_y * hx_dy
    e_x = e_x + e_coef * (hz_dy + psi_exy - hy_dz)
    e_y = e_y + e_coef * (hx_dz - hz_dx - psi_eyx)
    e_z = e_z + e_coef * (hy_dx + psi_ezx - hx_dy - psi_ezy)
    return (jnp.stack((e_x, e_y, e_z)), (psi_exy, psi_eyx, psi_ezx, psi_ezy))


def shards(e_field, h_field, e_coef, basis, pml_width, snap_index):
    depth_z, rows_here, cols_here = e_coef.shape
    full_x = rows_here * lax.axis_size(ROW)
    full_y = cols_here * lax.axis_size(COL)
    x_first = lax.axis_index(ROW) * rows_here
    y_first = lax.axis_index(COL) * cols_here
    widths = pml_width.astype(jnp.float32)
    x_pos = x_first.astype(jnp.float32) + jnp.arange(rows_here, dtype=jnp.float32)
    y_pos = y_first.astype(jnp.float32) + jnp.arange(cols_here, dtype=jnp.float32)
    hdx, hgx = absorber(x_pos + 0.5, float(full_x), widths[0], widths[1])
    hdy, hgy = absorber(y_pos + 0.5, float(full_y), widths[2], widths[3])
    edx, egx = absorber(x_pos, float(full_x), widths[0], widths[1])
    edy, egy = absorber(y_pos, float(full_y), widths[2], widths[3])
    hdx, hgx, edx, egx = [v.reshape(1, rows_here, 1) for v in (hdx, hgx, edx, egx)]
    hdy, hgy, edy, egy = [v.reshape(1, 1, cols_here) for v in (hdy, hgy, edy, egy)]
    zeros_cells = jnp.zeros((depth_z, rows_here, cols_here), jnp.float32)
    psi_mag = (zeros_cells,) * 4
    psi_ele = (zeros_cells,) * 4
    for step in range(STEPS):
        next_x = from_behind(e_field[1:3, :, 0, :], ROW, -1)
        next_y = from_behind(jnp.stack((e_field[0, :, :, 0], e_field[2, :, :, 0])), COL, -1)
        h_field, psi_mag = magnetic(e_field, h_field, psi_mag, next_x, next_y, hdx, hgx, hdy, hgy)
        prev_x = from_behind(h_field[1:3, :, -1, :], ROW, 1)
        prev_y = from_behind(jnp.stack((h_field[0, :, :, -1], h_field[2, :, :, -1])), COL, 1)
        e_field, psi_ele = electric(
            e_field, h_field, psi_ele, e_coef, prev_x, prev_y, edx, egx, edy, egy
        )
    planes = jnp.concatenate((e_field, h_field), 0).reshape(6 * depth_z, rows_here, cols_here)
    snaps = jnp.take(planes, snap_index, axis=0)
    count = snaps.shape[0]
    flat = snaps.reshape(count, rows_here * cols_here)
    gram_part = jnp.dot(flat, flat.T, precision=lax.Precision.HIGHEST) / float(full_x * full_y)
    local_modes = lax.all_to_all(basis, ROW, split_axis=1, concat_axis=0, tiled=True)
    coef_part = jnp.dot(
        flat, local_modes.reshape(local_modes.shape[0], -1).T, precision=lax.Precision.HIGHEST
    )
    coefficients, gram = (by_axis(coef_part, ROW_COL), by_axis(gram_part, ROW_COL))
    return (e_field, h_field, coefficients, gram)


def solution(mesh):
    split = Mesh(mesh.devices.reshape(4, 2, 8, 2, 2), ("row_0", "row_1", "col_0", "col_1", "col_2"))
    return jax.shard_map(
        shards,
        mesh=split,
        in_specs=(
            P(None, None, ROW, COL),
            P(None, None, ROW, COL),
            P(None, ROW, COL),
            P(ROW, None, COL),
            P(),
            P(),
        ),
        out_specs=(P(None, None, ROW, COL), P(None, None, ROW, COL), P(), P()),
        check_vma=False,
    )
```

profile of v0, /device:TPU:57, one launch (start us, length us, event | category | flops | bytes accessed | tf_op | source)
XLA Modules:
  0.0 416.7 jit_solution(7778291619104819544)
XLA Ops:
  1.8 2.9 collective-permute-start
  6.0 2.9 collective-permute-start.1
  10.0 7.2 %all-to-all-start = ((f32[16,64,128]{2,0,1:T(8,128)}), f32[16,64,128]{2,0,1:T(8,128)}, u32[]{:S(2)}, u32[]{:S(2)}) async-start(f32[16,64,128]{2,0,1:T(8,128)} %copy.1592), calls=%async_computation | async-start | bytes 1048576 | tf_op jit(solution)/shard_map/all_to_all | solution.py:126
  31.3 2.2 bitcast_subtract_fusion.1
  33.7 4.2 %collective-permute-start.2 = (f32[2,64,8]{1,2,0:T(8,128)S(1)}, f32[2,64,8]{1,2,0:T(8,128)S(1)}, u32[]{:S(2)}, u32[]{:S(2)}) collective-permute-start(f32[2,64,8]{1,2,0:T(8,128)S(1)} %pad_maximum_fusion.18), channel_id=1, source_target_pairs={{0,1},{1,2},{2,3},{3,4},{4,5},{5,6},{6,7},{7,8},{8,9},{9,10},{10,1... | collective-permute-start | bytes 12296 | tf_op jit(solution)/shard_map/ppermute | solution.py:19
  37.9 2.0 bitcast_subtract_fusion
  40.8 3.7 collective-permute-start.3
  47.3 2.0 multiply_add_fusion.69
  55.3 2.6 collective-permute-start.4
  59.6 3.3 collective-permute-done.4
  62.9 2.3 multiply_subtract_fusion.20
  65.5 2.4 multiply_subtract_fusion.19
  68.1 5.7 %collective-permute-start.6 = (f32[2,64,8]{1,2,0:T(8,128)S(1)}, f32[2,64,8]{1,2,0:T(8,128)S(1)}, u32[]{:S(2)}, u32[]{:S(2)}) collective-permute-start(f32[2,64,8]{1,2,0:T(8,128)S(1)} %pad_maximum_fusion.20), channel_id=1, source_target_pairs={{0,1},{1,2},{2,3},{3,4},{4,5},{5,6},{6,7},{7,8},{8,9},{9,10},{10,1... | collective-permute-start | bytes 12296 | tf_op jit(solution)/shard_map/ppermute | solution.py:19
  75.3 3.7 collective-permute-start.7
  84.2 2.0 multiply_add_fusion.55
  92.5 3.7 collective-permute-start.8
  101.9 2.3 multiply_subtract_fusion.17
  105.2 4.8 %collective-permute-start.10 = (f32[2,64,8]{1,2,0:T(8,128)S(1)}, f32[2,64,8]{1,2,0:T(8,128)S(1)}, u32[]{:S(2)}, u32[]{:S(2)}) collective-permute-start(f32[2,64,8]{1,2,0:T(8,128)S(1)} %pad_maximum_fusion.22), channel_id=1, source_target_pairs={{0,1},{1,2},{2,3},{3,4},{4,5},{5,6},{6,7},{7,8},{8,9},{9,10},{10,1... | collective-permute-start | bytes 12296 | tf_op jit(solution)/shard_map/ppermute | solution.py:19
  110.0 2.2 multiply_subtract_fusion.15
  113.6 4.6 %collective-permute-start.11 = (f32[2,64,128]{2,1,0:T(8,128)}, f32[2,64,128]{2,1,0:T(8,128)}, u32[]{:S(2)}, u32[]{:S(2)}) collective-permute-start(f32[2,64,128]{2,1,0:T(8,128)} %bitcast.74), channel_id=1, source_target_pairs={{0,32},{32,64},{64,96},{96,128},{128,160},{160,192},{192,224},{1,3... | collective-permute-start | bytes 196616 | tf_op jit(solution)/shard_map/ppermute | solution.py:19
  134.4 3.0 collective-permute-start.12
  138.3 2.3 multiply_subtract_fusion.13
  143.8 2.3 multiply_subtract_fusion.14
  147.2 4.7 %collective-permute-start.14 = (f32[2,64,8]{1,2,0:T(8,128)S(1)}, f32[2,64,8]{1,2,0:T(8,128)S(1)}, u32[]{:S(2)}, u32[]{:S(2)}) collective-permute-start(f32[2,64,8]{1,2,0:T(8,128)S(1)} %pad_maximum_fusion.24), channel_id=1, source_target_pairs={{0,1},{1,2},{2,3},{3,4},{4,5},{5,6},{6,7},{7,8},{8,9},{9,10},{10,1... | collective-permute-start | bytes 12296 | tf_op jit(solution)/shard_map/ppermute | solution.py:19
  154.6 5.6 %collective-permute-start.15 = (f32[2,64,128]{2,1,0:T(8,128)}, f32[2,64,128]{2,1,0:T(8,128)}, u32[]{:S(2)}, u32[]{:S(2)}) collective-permute-start(f32[2,64,128]{2,1,0:T(8,128)} %fusion.12), channel_id=1, source_target_pairs={{0,32},{32,64},{64,96},{96,128},{128,160},{160,192},{192,224},{1,3... | collective-permute-start | bytes 196616 | tf_op jit(solution)/shard_map/ppermute | solution.py:19
  163.0 2.1 multiply_add_fusion.38
  183.8 2.4 multiply_subtract_fusion.11
  187.1 5.7 %collective-permute-start.18 = (f32[2,64,8]{1,2,0:T(8,128)S(1)}, f32[2,64,8]{1,2,0:T(8,128)S(1)}, u32[]{:S(2)}, u32[]{:S(2)}) collective-permute-start(f32[2,64,8]{1,2,0:T(8,128)S(1)} %pad_maximum_fusion.26), channel_id=1, source_target_pairs={{0,1},{1,2},{2,3},{3,4},{4,5},{5,6},{6,7},{7,8},{8,9},{9,10},{10,1... | collective-permute-start | bytes 12296 | tf_op jit(solution)/shard_map/ppermute | solution.py:19
  192.8 2.1 multiply_subtract_fusion.9
  195.8 3.7 collective-permute-start.19
  217.4 3.6 collective-permute-start.20
  222.0 2.1 multiply_subtract_fusion.7
  227.4 2.3 multiply_subtract_fusion.8
  231.5 4.3 %collective-permute-start.22 = (f32[2,64,8]{1,2,0:T(8,128)S(1)}, f32[2,64,8]{1,2,0:T(8,128)S(1)}, u32[]{:S(2)}, u32[]{:S(2)}) collective-permute-start(f32[2,64,8]{1,2,0:T(8,128)S(1)} %pad_maximum_fusion.28), channel_id=1, source_target_pairs={{0,1},{1,2},{2,3},{3,4},{4,5},{5,6},{6,7},{7,8},{8,9},{9,10},{10,1... | collective-permute-start | bytes 12296 | tf_op jit(solution)/shard_map/ppermute | solution.py:19
  238.4 5.2 %collective-permute-start.23 = (f32[2,64,128]{2,1,0:T(8,128)}, f32[2,64,128]{2,1,0:T(8,128)}, u32[]{:S(2)}, u32[]{:S(2)}) collective-permute-start(f32[2,64,128]{2,1,0:T(8,128)} %fusion.9), channel_id=1, source_target_pairs={{0,32},{32,64},{64,96},{96,128},{128,160},{160,192},{192,224},{1,3... | collective-permute-start | bytes 196616 | tf_op jit(solution)/shard_map/ppermute | solution.py:19
  258.3 2.2 collective-permute-start.24
  270.7 5.7 %collective-permute-start.26 = (f32[2,64,8]{1,2,0:T(8,128)S(1)}, f32[2,64,8]{1,2,0:T(8,128)S(1)}, u32[]{:S(2)}, u32[]{:S(2)}) collective-permute-start(f32[2,64,8]{1,2,0:T(8,128)S(1)} %pad_maximum_fusion.30), channel_id=1, source_target_pairs={{0,1},{1,2},{2,3},{3,4},{4,5},{5,6},{6,7},{7,8},{8,9},{9,10},{10,1... | collective-permute-start | bytes 12296 | tf_op jit(solution)/shard_map/ppermute | solution.py:19
  276.4 2.1 multiply_subtract_fusion.3
  279.9 4.7 %collective-permute-start.27 = (f32[2,64,128]{2,1,0:T(8,128)}, f32[2,64,128]{2,1,0:T(8,128)}, u32[]{:S(2)}, u32[]{:S(2)}) collective-permute-start(f32[2,64,128]{2,1,0:T(8,128)} %fusion.8), channel_id=1, source_target_pairs={{0,32},{32,64},{64,96},{96,128},{128,160},{160,192},{192,224},{1,3... | collective-permute-start | bytes 196616 | tf_op jit(solution)/shard_map/ppermute | solution.py:19
  301.2 2.7 collective-permute-start.28
  312.5 5.7 %collective-permute-start.30 = (f32[2,64,8]{1,2,0:T(8,128)S(1)}, f32[2,64,8]{1,2,0:T(8,128)S(1)}, u32[]{:S(2)}, u32[]{:S(2)}) collective-permute-start(f32[2,64,8]{1,2,0:T(8,128)S(1)} %pad_maximum_fusion.32), channel_id=1, source_target_pairs={{0,1},{1,2},{2,3},{3,4},{4,5},{5,6},{6,7},{7,8},{8,9},{9,10},{10,1... | collective-permute-start | bytes 12296 | tf_op jit(solution)/shard_map/ppermute | solution.py:19
  321.1 4.6 %collective-permute-start.31 = (f32[2,64,128]{2,1,0:T(8,128)S(1)}, f32[2,64,128]{2,1,0:T(8,128)}, u32[]{:S(2)}, u32[]{:S(2)}) collective-permute-start(f32[2,64,128]{2,1,0:T(8,128)S(1)} %bitcast.520), channel_id=1, source_target_pairs={{0,32},{32,64},{64,96},{96,128},{128,160},{160,192},{192,224},{1,3... | collective-permute-start | bytes 196616 | tf_op jit(solution)/shard_map/ppermute | solution.py:19
  334.4 2.1 gather_fusion
  337.7 12.6 %all-reduce.33 = (f32[64,128]{1,0:T(8,128)S(1)}, f32[64,64]{1,0:T(8,128)S(1)}) all-reduce(f32[64,128]{1,0:T(8,128)S(1)} %fusion.1, f32[64,64]{1,0:T(8,128)S(1)} %fusion), channel_id=1, replica_groups=mesh['row_0'=4,'row_1'=2,'col_0'=8,'col_1'=2,'col_2'=2] {'row_0'}, use_global_device_ids=true, to_apply=%region_0.1 | all-reduce | flops 12288 | bytes 98304 | tf_op jit(solution)/shard_map/psum | solution.py:24
  350.3 10.4 %all-reduce.36 = (f32[64,128]{1,0:T(8,128)S(1)}, f32[64,64]{1,0:T(8,128)S(1)}) all-reduce(f32[64,128]{1,0:T(8,128)S(1)} %get-tuple-element.18, f32[64,64]{1,0:T(8,128)S(1)} %get-tuple-element.19), channel_id=1, replica_groups=mesh['row_0'=4,'row_1'=2,'col_0'=8,'col_1'=2,'col_2'=2] {'row_1'}, use_global_device_ids=true, to_apply=%region_1.2 | all-reduce | flops 12288 | bytes 98304 | tf_op jit(solution)/shard_map/psum | solution.py:24
  360.7 31.1 %all-reduce.32 = (f32[64,128]{1,0:T(8,128)S(1)}, f32[64,64]{1,0:T(8,128)S(1)}) all-reduce(f32[64,128]{1,0:T(8,128)S(1)} %get-tuple-element.24, f32[64,64]{1,0:T(8,128)S(1)} %get-tuple-element.25), channel_id=1, replica_groups=mesh['row_0'=4,'row_1'=2,'col_0'=8,'col_1'=2,'col_2'=2] {'col_0'}, use_global_device_ids=true, to_apply=%region_2.3 | all-reduce | flops 12288 | bytes 98304 | tf_op jit(solution)/shard_map/psum | solution.py:24
  391.9 5.6 %all-reduce.35 = (f32[64,128]{1,0:T(8,128)S(1)}, f32[64,64]{1,0:T(8,128)S(1)}) all-reduce(f32[64,128]{1,0:T(8,128)S(1)} %get-tuple-element.16, f32[64,64]{1,0:T(8,128)S(1)} %get-tuple-element.17), channel_id=1, replica_groups=mesh['row_0'=4,'row_1'=2,'col_0'=8,'col_1'=2,'col_2'=2] {'col_1'}, use_global_device_ids=true, to_apply=%region_3.4 | all-reduce | flops 12288 | bytes 98304 | tf_op jit(solution)/shard_map/psum | solution.py:24
  397.5 18.3 %all-reduce.34 = (f32[64,128]{1,0:T(8,128)}, f32[64,64]{1,0:T(8,128)}) all-reduce(f32[64,128]{1,0:T(8,128)S(1)} %get-tuple-element.22, f32[64,64]{1,0:T(8,128)S(1)} %get-tuple-element.23), channel_id=1, replica_groups=mesh['row_0'=4,'row_1'=2,'col_0'=8,'col_1'=2,'col_2'=2] {'col_2'}, use_global_device_ids=true, to_apply=%region_4.5 | all-reduce | flops 12288 | bytes 98304 | tf_op jit(solution)/shard_map/psum | solution.py:24
  (543 shorter events, 186.8 us)
Async XLA Ops:
  1.8 26.6 %collective-permute-start = (f32[2,64,128]{2,1,0:T(8,128)S(1)}, f32[2,64,128]{2,1,0:T(8,128)}, u32[]{:S(2)}, u32[]{:S(2)}) collective-permute-start(f32[2,64,128]{2,1,0:T(8,128)S(1)} %bitcast.522), channel_id=1, source_target_pairs={{32,0},{64,32},{96,64},{128,96},{160,128},{192,160},{224,192},{33,... | collective-permute-start | bytes 196616 | tf_op jit(solution)/shard_map/ppermute | solution.py:19
  5.7 11.5 %copy-start.1 = (f32[3,64,8,128]{3,2,1,0:T(8,128)S(1)}, f32[3,64,8,128]{3,2,1,0:T(8,128)}, u32[]{:S(2)}) copy-start(f32[3,64,8,128]{3,2,1,0:T(8,128)} %param.6) | copy-start | bytes 2359300
  6.0 21.1 %collective-permute-start.1 = (f32[2,64,8]{1,2,0:T(8,128)S(1)}, f32[2,64,8]{1,2,0:T(8,128)S(1)}, u32[]{:S(2)}, u32[]{:S(2)}) collective-permute-start(f32[2,64,8]{1,2,0:T(8,128)S(1)} %pad_maximum_fusion.17), channel_id=1, source_target_pairs={{1,0},{2,1},{3,2},{4,3},{5,4},{6,5},{7,6},{8,7},{9,8},{10,9},{11,1... | collective-permute-start | bytes 12296 | tf_op jit(solution)/shard_map/ppermute | solution.py:19
  10.0 15.6 %copy-start.109 = (s32[64]{0:T(128)S(1)}, s32[64]{0:T(128)}, u32[]{:S(2)}) copy-start(s32[64]{0:T(128)} %param.11) | copy-start | bytes 772
  10.0 150.1 %all-to-all-start = ((f32[16,64,128]{2,0,1:T(8,128)}), f32[16,64,128]{2,0,1:T(8,128)}, u32[]{:S(2)}, u32[]{:S(2)}) async-start(f32[16,64,128]{2,0,1:T(8,128)} %copy.1592), calls=%async_computation | async-start | bytes 1048576 | tf_op jit(solution)/shard_map/all_to_all | solution.py:126
  22.0 25.3 %copy-start.98 = (f32[128]{0:T(128)}, f32[128]{0:T(128)S(1)}, u32[]{:S(2)}) copy-start(f32[128]{0:T(128)S(1)} %get-tuple-element.88) | copy-start | bytes 1540
  23.9 14.0 %copy-start.101 = (f32[8]{0:T(128)}, f32[8]{0:T(128)S(1)}, u32[]{:S(2)}) copy-start(f32[8]{0:T(128)S(1)} %get-tuple-element.94) | copy-start | bytes 100
  26.5 20.8 %copy-start.68 = (f32[8]{0:T(128)}, f32[8]{0:T(128)S(1)}, u32[]{:S(2)}) copy-start(f32[8]{0:T(128)S(1)} %fusion.20) | copy-start | bytes 100
  33.5 32.0 %copy-start.6 = (f32[64,8,128]{2,1,0:T(8,128)}, f32[64,8,128]{2,1,0:T(8,128)S(1)}, u32[]{:S(2)}) copy-start(f32[64,8,128]{2,1,0:T(8,128)S(1)} %get-tuple-element.98) | copy-start | bytes 786436
  33.7 10.7 %collective-permute-start.2 = (f32[2,64,8]{1,2,0:T(8,128)S(1)}, f32[2,64,8]{1,2,0:T(8,128)S(1)}, u32[]{:S(2)}, u32[]{:S(2)}) collective-permute-start(f32[2,64,8]{1,2,0:T(8,128)S(1)} %pad_maximum_fusion.18), channel_id=1, source_target_pairs={{0,1},{1,2},{2,3},{3,4},{4,5},{5,6},{6,7},{7,8},{8,9},{9,10},{10,1... | collective-permute-start | bytes 12296 | tf_op jit(solution)/shard_map/ppermute | solution.py:19
  40.8 6.5 %collective-permute-start.3 = (f32[2,64,128]{2,1,0:T(8,128)S(1)}, f32[2,64,128]{2,1,0:T(8,128)S(1)}, u32[]{:S(2)}, u32[]{:S(2)}) collective-permute-start(f32[2,64,128]{2,1,0:T(8,128)S(1)} %bitcast.519), channel_id=1, source_target_pairs={{0,32},{32,64},{64,96},{96,128},{128,160},{160,192},{192,224},{1,3... | collective-permute-start | bytes 196616 | tf_op jit(solution)/shard_map/ppermute | solution.py:19
  49.6 8.3 %collective-permute-start.5 = (f32[2,64,8]{1,2,0:T(8,128)S(1)}, f32[2,64,8]{1,2,0:T(8,128)S(1)}, u32[]{:S(2)}, u32[]{:S(2)}) collective-permute-start(f32[2,64,8]{1,2,0:T(8,128)S(1)} %pad_maximum_fusion.19), channel_id=1, source_target_pairs={{1,0},{2,1},{3,2},{4,3},{5,4},{6,5},{7,6},{8,7},{9,8},{10,9},{11,1... | collective-permute-start | bytes 12296 | tf_op jit(solution)/shard_map/ppermute | solution.py:19
  55.3 7.6 %collective-permute-start.4 = (f32[2,64,128]{2,1,0:T(8,128)}, f32[2,64,128]{2,1,0:T(8,128)S(1)}, u32[]{:S(2)}, u32[]{:S(2)}) collective-permute-start(f32[2,64,128]{2,1,0:T(8,128)} %fusion.16), channel_id=1, source_target_pairs={{32,0},{64,32},{96,64},{128,96},{160,128},{192,160},{224,192},{33,... | collective-permute-start | bytes 196616 | tf_op jit(solution)/shard_map/ppermute | solution.py:19
  67.9 11.3 %copy-start.76 = (f32[128]{0:T(128)S(1)}, f32[128]{0:T(128)}, u32[]{:S(2)}) copy-start(f32[128]{0:T(128)} %copy-done.75) | copy-start | bytes 1540
  67.9 11.3 %copy-start.99 = (f32[128]{0:T(128)S(1)}, f32[128]{0:T(128)}, u32[]{:S(2)}) copy-start(f32[128]{0:T(128)} %copy-done.98) | copy-start | bytes 1540
  68.1 10.8 %collective-permute-start.6 = (f32[2,64,8]{1,2,0:T(8,128)S(1)}, f32[2,64,8]{1,2,0:T(8,128)S(1)}, u32[]{:S(2)}, u32[]{:S(2)}) collective-permute-start(f32[2,64,8]{1,2,0:T(8,128)S(1)} %pad_maximum_fusion.20), channel_id=1, source_target_pairs={{0,1},{1,2},{2,3},{3,4},{4,5},{5,6},{6,7},{7,8},{8,9},{9,10},{10,1... | collective-permute-start | bytes 12296 | tf_op jit(solution)/shard_map/ppermute | solution.py:19
  75.3 8.0 %collective-permute-start.7 = (f32[2,64,128]{2,1,0:T(8,128)}, f32[2,64,128]{2,1,0:T(8,128)}, u32[]{:S(2)}, u32[]{:S(2)}) collective-permute-start(f32[2,64,128]{2,1,0:T(8,128)} %fusion.15), channel_id=1, source_target_pairs={{0,32},{32,64},{64,96},{96,128},{128,160},{160,192},{192,224},{1,3... | collective-permute-start | bytes 196616 | tf_op jit(solution)/shard_map/ppermute | solution.py:19
  86.9 9.3 %collective-permute-start.9 = (f32[2,64,8]{1,2,0:T(8,128)S(1)}, f32[2,64,8]{1,2,0:T(8,128)S(1)}, u32[]{:S(2)}, u32[]{:S(2)}) collective-permute-start(f32[2,64,8]{1,2,0:T(8,128)S(1)} %pad_maximum_fusion.21), channel_id=1, source_target_pairs={{1,0},{2,1},{3,2},{4,3},{5,4},{6,5},{7,6},{8,7},{9,8},{10,9},{11,1... | collective-permute-start | bytes 12296 | tf_op jit(solution)/shard_map/ppermute | solution.py:19
  92.5 8.6 %collective-permute-start.8 = (f32[2,64,128]{2,1,0:T(8,128)}, f32[2,64,128]{2,1,0:T(8,128)}, u32[]{:S(2)}, u32[]{:S(2)}) collective-permute-start(f32[2,64,128]{2,1,0:T(8,128)} %fusion.14), channel_id=1, source_target_pairs={{32,0},{64,32},{96,64},{128,96},{160,128},{192,160},{224,192},{33,... | collective-permute-start | bytes 196616 | tf_op jit(solution)/shard_map/ppermute | solution.py:19
  105.2 13.0 %collective-permute-start.10 = (f32[2,64,8]{1,2,0:T(8,128)S(1)}, f32[2,64,8]{1,2,0:T(8,128)S(1)}, u32[]{:S(2)}, u32[]{:S(2)}) collective-permute-start(f32[2,64,8]{1,2,0:T(8,128)S(1)} %pad_maximum_fusion.22), channel_id=1, source_target_pairs={{0,1},{1,2},{2,3},{3,4},{4,5},{5,6},{6,7},{7,8},{8,9},{9,10},{10,1... | collective-permute-start | bytes 12296 | tf_op jit(solution)/shard_map/ppermute | solution.py:19
  113.6 9.4 %collective-permute-start.11 = (f32[2,64,128]{2,1,0:T(8,128)}, f32[2,64,128]{2,1,0:T(8,128)}, u32[]{:S(2)}, u32[]{:S(2)}) collective-permute-start(f32[2,64,128]{2,1,0:T(8,128)} %bitcast.74), channel_id=1, source_target_pairs={{0,32},{32,64},{64,96},{96,128},{128,160},{160,192},{192,224},{1,3... | collective-permute-start | bytes 196616 | tf_op jit(solution)/shard_map/ppermute | solution.py:19
  125.3 43.2 %copy-start.13 = (f32[64,8,128]{2,1,0:T(8,128)}, f32[64,8,128]{2,1,0:T(8,128)S(1)}, u32[]{:S(2)}) copy-start(f32[64,8,128]{2,1,0:T(8,128)S(1)} %get-tuple-element.65) | copy-start | bytes 786436
  128.0 9.4 %collective-permute-start.13 = (f32[2,64,8]{1,2,0:T(8,128)S(1)}, f32[2,64,8]{1,2,0:T(8,128)S(1)}, u32[]{:S(2)}, u32[]{:S(2)}) collective-permute-start(f32[2,64,8]{1,2,0:T(8,128)S(1)} %pad_maximum_fusion.23), channel_id=1, source_target_pairs={{1,0},{2,1},{3,2},{4,3},{5,4},{6,5},{7,6},{8,7},{9,8},{10,9},{11,1... | collective-permute-start | bytes 12296 | tf_op jit(solution)/shard_map/ppermute | solution.py:19
  134.4 8.7 %collective-permute-start.12 = (f32[2,64,128]{2,1,0:T(8,128)}, f32[2,64,128]{2,1,0:T(8,128)}, u32[]{:S(2)}, u32[]{:S(2)}) collective-permute-start(f32[2,64,128]{2,1,0:T(8,128)} %fusion.13), channel_id=1, source_target_pairs={{32,0},{64,32},{96,64},{128,96},{160,128},{192,160},{224,192},{33,... | collective-permute-start | bytes 196616 | tf_op jit(solution)/shard_map/ppermute | solution.py:19
  147.2 15.0 %collective-permute-start.14 = (f32[2,64,8]{1,2,0:T(8,128)S(1)}, f32[2,64,8]{1,2,0:T(8,128)S(1)}, u32[]{:S(2)}, u32[]{:S(2)}) collective-permute-start(f32[2,64,8]{1,2,0:T(8,128)S(1)} %pad_maximum_fusion.24), channel_id=1, source_target_pairs={{0,1},{1,2},{2,3},{3,4},{4,5},{5,6},{6,7},{7,8},{8,9},{9,10},{10,1... | collective-permute-start | bytes 12296 | tf_op jit(solution)/shard_map/ppermute | solution.py:19
  154.6 13.1 %collective-permute-start.15 = (f32[2,64,128]{2,1,0:T(8,128)}, f32[2,64,128]{2,1,0:T(8,128)}, u32[]{:S(2)}, u32[]{:S(2)}) collective-permute-start(f32[2,64,128]{2,1,0:T(8,128)} %fusion.12), channel_id=1, source_target_pairs={{0,32},{32,64},{64,96},{96,128},{128,160},{160,192},{192,224},{1,3... | collective-permute-start | bytes 196616 | tf_op jit(solution)/shard_map/ppermute | solution.py:19
  171.0 6.2 %collective-permute-start.17 = (f32[2,64,8]{1,2,0:T(8,128)S(1)}, f32[2,64,8]{1,2,0:T(8,128)S(1)}, u32[]{:S(2)}, u32[]{:S(2)}) collective-permute-start(f32[2,64,8]{1,2,0:T(8,128)S(1)} %pad_maximum_fusion.25), channel_id=1, source_target_pairs={{1,0},{2,1},{3,2},{4,3},{5,4},{6,5},{7,6},{8,7},{9,8},{10,9},{11,1... | collective-permute-start | bytes 12296 | tf_op jit(solution)/shard_map/ppermute | solution.py:19
  175.2 7.7 %collective-permute-start.16 = (f32[2,64,128]{2,1,0:T(8,128)}, f32[2,64,128]{2,1,0:T(8,128)}, u32[]{:S(2)}, u32[]{:S(2)}) collective-permute-start(f32[2,64,128]{2,1,0:T(8,128)} %fusion.11), channel_id=1, source_target_pairs={{32,0},{64,32},{96,64},{128,96},{160,128},{192,160},{224,192},{33,... | collective-permute-start | bytes 196616 | tf_op jit(solution)/shard_map/ppermute | solution.py:19
  187.1 12.4 %collective-permute-start.18 = (f32[2,64,8]{1,2,0:T(8,128)S(1)}, f32[2,64,8]{1,2,0:T(8,128)S(1)}, u32[]{:S(2)}, u32[]{:S(2)}) collective-permute-start(f32[2,64,8]{1,2,0:T(8,128)S(1)} %pad_maximum_fusion.26), channel_id=1, source_target_pairs={{0,1},{1,2},{2,3},{3,4},{4,5},{5,6},{6,7},{7,8},{8,9},{9,10},{10,1... | collective-permute-start | bytes 12296 | tf_op jit(solution)/shard_map/ppermute | solution.py:19
  195.8 9.7 %collective-permute-start.19 = (f32[2,64,128]{2,1,0:T(8,128)S(1)}, f32[2,64,128]{2,1,0:T(8,128)}, u32[]{:S(2)}, u32[]{:S(2)}) collective-permute-start(f32[2,64,128]{2,1,0:T(8,128)S(1)} %bitcast.521), channel_id=1, source_target_pairs={{0,32},{32,64},{64,96},{96,128},{128,160},{160,192},{192,224},{1,3... | collective-permute-start | bytes 196616 | tf_op jit(solution)/shard_map/ppermute | solution.py:19
  210.1 11.8 %copy-start.46 = (f32[64,8,127]{2,1,0:T(8,128)S(1)}, f32[64,8,127]{2,1,0:T(8,128)}, u32[]{:S(2)}) copy-start(f32[64,8,127]{2,1,0:T(8,128)} %copy-done.45) | copy-start | bytes 780292
  210.1 11.8 %copy-start.48 = (f32[64,8,1]{2,1,0:T(8,128)S(1)}, f32[64,8,1]{2,1,0:T(8,128)}, u32[]{:S(2)}) copy-start(f32[64,8,1]{2,1,0:T(8,128)} %copy-done.47) | copy-start | bytes 6148
  210.1 11.8 %copy-start.51 = (f32[64,8,128]{2,1,0:T(8,128)S(1)}, f32[64,8,128]{2,1,0:T(8,128)}, u32[]{:S(2)}) copy-start(f32[64,8,128]{2,1,0:T(8,128)} %get-tuple-element.59) | copy-start | bytes 786436
  210.1 11.8 %copy-start.92 = (f32[128]{0:T(128)S(1)}, f32[128]{0:T(128)}, u32[]{:S(2)}) copy-start(f32[128]{0:T(128)} %copy-done.88) | copy-start | bytes 1540
  211.1 10.0 %collective-permute-start.21 = (f32[2,64,8]{1,2,0:T(8,128)S(1)}, f32[2,64,8]{1,2,0:T(8,128)S(1)}, u32[]{:S(2)}, u32[]{:S(2)}) collective-permute-start(f32[2,64,8]{1,2,0:T(8,128)S(1)} %pad_maximum_fusion.27), channel_id=1, source_target_pairs={{1,0},{2,1},{3,2},{4,3},{5,4},{6,5},{7,6},{8,7},{9,8},{10,9},{11,1... | collective-permute-start | bytes 12296 | tf_op jit(solution)/shard_map/ppermute | solution.py:19
  217.4 9.1 %collective-permute-start.20 = (f32[2,64,128]{2,1,0:T(8,128)}, f32[2,64,128]{2,1,0:T(8,128)}, u32[]{:S(2)}, u32[]{:S(2)}) collective-permute-start(f32[2,64,128]{2,1,0:T(8,128)} %fusion.10), channel_id=1, source_target_pairs={{32,0},{64,32},{96,64},{128,96},{160,128},{192,160},{224,192},{33,... | collective-permute-start | bytes 196616 | tf_op jit(solution)/shard_map/ppermute | solution.py:19
  231.5 12.1 %collective-permute-start.22 = (f32[2,64,8]{1,2,0:T(8,128)S(1)}, f32[2,64,8]{1,2,0:T(8,128)S(1)}, u32[]{:S(2)}, u32[]{:S(2)}) collective-permute-start(f32[2,64,8]{1,2,0:T(8,128)S(1)} %pad_maximum_fusion.28), channel_id=1, source_target_pairs={{0,1},{1,2},{2,3},{3,4},{4,5},{5,6},{6,7},{7,8},{8,9},{9,10},{10,1... | collective-permute-start | bytes 12296 | tf_op jit(solution)/shard_map/ppermute | solution.py:19
  238.4 9.8 %collective-permute-start.23 = (f32[2,64,128]{2,1,0:T(8,128)}, f32[2,64,128]{2,1,0:T(8,128)}, u32[]{:S(2)}, u32[]{:S(2)}) collective-permute-start(f32[2,64,128]{2,1,0:T(8,128)} %fusion.9), channel_id=1, source_target_pairs={{0,32},{32,64},{64,96},{96,128},{128,160},{160,192},{192,224},{1,3... | collective-permute-start | bytes 196616 | tf_op jit(solution)/shard_map/ppermute | solution.py:19
  251.6 8.9 %collective-permute-start.25 = (f32[2,64,8]{1,2,0:T(8,128)S(1)}, f32[2,64,8]{1,2,0:T(8,128)S(1)}, u32[]{:S(2)}, u32[]{:S(2)}) collective-permute-start(f32[2,64,8]{1,2,0:T(8,128)S(1)} %pad_maximum_fusion.29), channel_id=1, source_target_pairs={{1,0},{2,1},{3,2},{4,3},{5,4},{6,5},{7,6},{8,7},{9,8},{10,9},{11,1... | collective-permute-start | bytes 12296 | tf_op jit(solution)/shard_map/ppermute | solution.py:19
  258.3 7.7 %collective-permute-start.24 = (f32[2,64,128]{2,1,0:T(8,128)}, f32[2,64,128]{2,1,0:T(8,128)}, u32[]{:S(2)}, u32[]{:S(2)}) collective-permute-start(f32[2,64,128]{2,1,0:T(8,128)} %bitcast.148), channel_id=1, source_target_pairs={{32,0},{64,32},{96,64},{128,96},{160,128},{192,160},{224,192},{33,... | collective-permute-start | bytes 196616 | tf_op jit(solution)/shard_map/ppermute | solution.py:19
  270.7 13.9 %collective-permute-start.26 = (f32[2,64,8]{1,2,0:T(8,128)S(1)}, f32[2,64,8]{1,2,0:T(8,128)S(1)}, u32[]{:S(2)}, u32[]{:S(2)}) collective-permute-start(f32[2,64,8]{1,2,0:T(8,128)S(1)} %pad_maximum_fusion.30), channel_id=1, source_target_pairs={{0,1},{1,2},{2,3},{3,4},{4,5},{5,6},{6,7},{7,8},{8,9},{9,10},{10,1... | collective-permute-start | bytes 12296 | tf_op jit(solution)/shard_map/ppermute | solution.py:19
  279.9 10.1 %collective-permute-start.27 = (f32[2,64,128]{2,1,0:T(8,128)}, f32[2,64,128]{2,1,0:T(8,128)}, u32[]{:S(2)}, u32[]{:S(2)}) collective-permute-start(f32[2,64,128]{2,1,0:T(8,128)} %fusion.8), channel_id=1, source_target_pairs={{0,32},{32,64},{64,96},{96,128},{128,160},{160,192},{192,224},{1,3... | collective-permute-start | bytes 196616 | tf_op jit(solution)/shard_map/ppermute | solution.py:19
  294.8 9.1 %collective-permute-start.29 = (f32[2,64,8]{1,2,0:T(8,128)S(1)}, f32[2,64,8]{1,2,0:T(8,128)S(1)}, u32[]{:S(2)}, u32[]{:S(2)}) collective-permute-start(f32[2,64,8]{1,2,0:T(8,128)S(1)} %pad_maximum_fusion.31), channel_id=1, source_target_pairs={{1,0},{2,1},{3,2},{4,3},{5,4},{6,5},{7,6},{8,7},{9,8},{10,9},{11,1... | collective-permute-start | bytes 12296 | tf_op jit(solution)/shard_map/ppermute | solution.py:19
  301.2 7.7 %collective-permute-start.28 = (f32[2,64,128]{2,1,0:T(8,128)}, f32[2,64,128]{2,1,0:T(8,128)}, u32[]{:S(2)}, u32[]{:S(2)}) collective-permute-start(f32[2,64,128]{2,1,0:T(8,128)} %fusion.7), channel_id=1, source_target_pairs={{32,0},{64,32},{96,64},{128,96},{160,128},{192,160},{224,192},{33,... | collective-permute-start | bytes 196616 | tf_op jit(solution)/shard_map/ppermute | solution.py:19
  312.5 13.3 %collective-permute-start.30 = (f32[2,64,8]{1,2,0:T(8,128)S(1)}, f32[2,64,8]{1,2,0:T(8,128)S(1)}, u32[]{:S(2)}, u32[]{:S(2)}) collective-permute-start(f32[2,64,8]{1,2,0:T(8,128)S(1)} %pad_maximum_fusion.32), channel_id=1, source_target_pairs={{0,1},{1,2},{2,3},{3,4},{4,5},{5,6},{6,7},{7,8},{8,9},{9,10},{10,1... | collective-permute-start | bytes 12296 | tf_op jit(solution)/shard_map/ppermute | solution.py:19
  321.1 7.1 %collective-permute-start.31 = (f32[2,64,128]{2,1,0:T(8,128)S(1)}, f32[2,64,128]{2,1,0:T(8,128)}, u32[]{:S(2)}, u32[]{:S(2)}) collective-permute-start(f32[2,64,128]{2,1,0:T(8,128)S(1)} %bitcast.520), channel_id=1, source_target_pairs={{0,32},{32,64},{64,96},{96,128},{128,160},{160,192},{192,224},{1,3... | collective-permute-start | bytes 196616 | tf_op jit(solution)/shard_map/ppermute | solution.py:19
  333.7 82.1 %copy-start.58 = (f32[1,64,8,128]{3,2,1,0:T(8,128)S(1)}, f32[1,64,8,128]{3,2,1,0:T(8,128)}, u32[]{:S(2)}) copy-start(f32[1,64,8,128]{3,2,1,0:T(8,128)} %get-tuple-element.31) | copy-start | bytes 786436
  333.7 82.1 %copy-start.59 = (f32[1,64,8,128]{3,2,1,0:T(8,128)S(1)}, f32[1,64,8,128]{3,2,1,0:T(8,128)}, u32[]{:S(2)}) copy-start(f32[1,64,8,128]{3,2,1,0:T(8,128)} %get-tuple-element.29) | copy-start | bytes 786436
  (95 other events, 492.6 us)
where the time goes:
time: 420 us; the launch traced here: 417 us
  starting transfers between devices  122 us (29%)
  local copies, waits for them, and re-layouts  106 us (25%)
  other arithmetic  98.7 us (24%)
  blocking collectives  78 us (19%)
  waiting for transfers between devices  6.47 us (2%)
    ppermute x32, starting transfers between devices, from_behind(): return lax.ppermute(block, axis, route)  115 us
    psum x5, blocking collectives, by_axis(): array = lax.psum(array, axis)  78 us
    slice x45, local copies, waits for them, and re-layouts, forward(): lax.slice_in_dim(field, 1, count, axis=axis)  33.4 us
    sub x8, other arithmetic, magnetic(): h_z = h_z - time_step * (ey_dx + psi_hzx - ex_dy - psi_hzy)  15.1 us
    sub x8, other arithmetic, magnetic(): h_x = h_x - time_step * (ez_dy + psi_hxy - ey_dz)  14.7 us
    another operation x24, local copies, waits for them, and re-layouts, forward(): jnp.expand_dims(plane, axis)  12.5 us
    sub x7, other arithmetic, magnetic(): h_y = h_y - time_step * (ex_dz - ez_dx - psi_hyx)  12 us
    add x6, other arithmetic, electric(): e_z = e_z + e_coef * (hy_dx + psi_ezx - hx_dy - psi_ezy)  10.3 us
  transfers between devices with their start and end apart: 33, of which 5 were waited for; matrix products, arithmetic and copies ran while one was open for 38% of the time, Pallas kernels for 0%

commit v1 on v0

--- a/solution.py
+++ b/solution.py
@@ -21,7 +21,7 @@
 
 def by_axis(array, axes):
     for axis in axes:
-        array = lax.psum(array, axis)
+        array = jnp.sum(lax.all_gather(array, axis), axis=0)
     return array
 
 

time: 420 us -> 455 us (1.083)
  the two profiles are of different devices: /device:TPU:57 before, /device:TPU:1 now
where the time goes in v1:
time: 455 us; the launch traced here: 451 us
  starting transfers between devices  119 us (26%)
  blocking collectives  114 us (25%)
  local copies, waits for them, and re-layouts  106 us (23%)
  other arithmetic  100 us (22%)
  waiting for transfers between devices  7.47 us (2%)
    all_gather x10, blocking collectives, by_axis(): array = jnp.sum(lax.all_gather(array, axis), axis=0)  114 us
    ppermute x32, starting transfers between devices, from_behind(): return lax.ppermute(block, axis, route)  112 us
    slice x45, local copies, waits for them, and re-layouts, forward(): lax.slice_in_dim(field, 1, count, axis=axis)  33.3 us
    sub x8, other arithmetic, magnetic(): h_z = h_z - time_step * (ey_dx + psi_hzx - ex_dy - psi_hzy)  15.1 us
    sub x8, other arithmetic, magnetic(): h_x = h_x - time_step * (ez_dy + psi_hxy - ey_dz)  14.6 us
    another operation x24, local copies, waits for them, and re-layouts, forward(): jnp.expand_dims(plane, axis)  12.5 us
    sub x7, other arithmetic, magnetic(): h_y = h_y - time_step * (ex_dz - ez_dx - psi_hyx)  12 us
    add x6, other arithmetic, electric(): e_z = e_z + e_coef * (hy_dx + psi_ezx - hx_dy - psi_ezy)  10.3 us
  transfers between devices with their start and end apart: 33, of which 5 were waited for; matrix products, arithmetic and copies ran while one was open for 35% of the time, Pallas kernels for 0%

profile of v1, /device:TPU:1, one launch (start us, length us, event | category | flops | bytes accessed | tf_op | source)
XLA Modules:
  0.0 451.0 jit_solution(3161733578541423559)
XLA Ops:
  4.5 5.1 %collective-permute-start.1 = (f32[2,64,8]{1,2,0:T(8,128)S(1)}, f32[2,64,8]{1,2,0:T(8,128)S(1)}, u32[]{:S(2)}, u32[]{:S(2)}) collective-permute-start(f32[2,64,8]{1,2,0:T(8,128)S(1)} %pad_maximum_fusion.17), channel_id=1, source_target_pairs={{1,0},{2,1},{3,2},{4,3},{5,4},{6,5},{7,6},{8,7},{9,8},{10,9},{11,1... | collective-permute-start | bytes 12296 | tf_op jit(solution)/shard_map/ppermute | solution.py:19
  10.7 6.4 %all-to-all-start = ((f32[16,64,128]{2,0,1:T(8,128)}), f32[16,64,128]{2,0,1:T(8,128)}, u32[]{:S(2)}, u32[]{:S(2)}) async-start(f32[16,64,128]{2,0,1:T(8,128)} %copy.1826), calls=%async_computation | async-start | bytes 1048576 | tf_op jit(solution)/shard_map/all_to_all | solution.py:126
  31.1 2.2 bitcast_subtract_fusion.1
  33.6 3.4 collective-permute-start.2
  37.0 2.0 bitcast_subtract_fusion
  39.8 5.7 %collective-permute-start.3 = (f32[2,64,128]{2,1,0:T(8,128)S(1)}, f32[2,64,128]{2,1,0:T(8,128)S(1)}, u32[]{:S(2)}, u32[]{:S(2)}) collective-permute-start(f32[2,64,128]{2,1,0:T(8,128)S(1)} %bitcast.539), channel_id=1, source_target_pairs={{0,32},{32,64},{64,96},{96,128},{128,160},{160,192},{192,224},{1,3... | collective-permute-start | bytes 196616 | tf_op jit(solution)/shard_map/ppermute | solution.py:19
  47.9 2.0 multiply_add_fusion.69
  58.9 3.7 collective-permute-done.4
  62.6 2.3 multiply_subtract_fusion.20
  65.2 2.4 multiply_subtract_fusion.19
  67.8 4.8 %collective-permute-start.6 = (f32[2,64,8]{1,2,0:T(8,128)S(1)}, f32[2,64,8]{1,2,0:T(8,128)S(1)}, u32[]{:S(2)}, u32[]{:S(2)}) collective-permute-start(f32[2,64,8]{1,2,0:T(8,128)S(1)} %pad_maximum_fusion.20), channel_id=1, source_target_pairs={{0,1},{1,2},{2,3},{3,4},{4,5},{5,6},{6,7},{7,8},{8,9},{9,10},{10,1... | collective-permute-start | bytes 12296 | tf_op jit(solution)/shard_map/ppermute | solution.py:19
  74.1 5.9 %collective-permute-start.7 = (f32[2,64,128]{2,1,0:T(8,128)}, f32[2,64,128]{2,1,0:T(8,128)}, u32[]{:S(2)}, u32[]{:S(2)}) collective-permute-start(f32[2,64,128]{2,1,0:T(8,128)} %fusion.15), channel_id=1, source_target_pairs={{0,32},{32,64},{64,96},{96,128},{128,160},{160,192},{192,224},{1,3... | collective-permute-start | bytes 196616 | tf_op jit(solution)/shard_map/ppermute | solution.py:19
  85.1 2.0 multiply_add_fusion.55
  101.1 2.4 multiply_subtract_fusion.17
  104.4 5.1 %collective-permute-start.10 = (f32[2,64,8]{1,2,0:T(8,128)S(1)}, f32[2,64,8]{1,2,0:T(8,128)S(1)}, u32[]{:S(2)}, u32[]{:S(2)}) collective-permute-start(f32[2,64,8]{1,2,0:T(8,128)S(1)} %pad_maximum_fusion.22), channel_id=1, source_target_pairs={{0,1},{1,2},{2,3},{3,4},{4,5},{5,6},{6,7},{7,8},{8,9},{9,10},{10,1... | collective-permute-start | bytes 12296 | tf_op jit(solution)/shard_map/ppermute | solution.py:19
  109.5 2.1 multiply_subtract_fusion.15
  113.0 4.9 %collective-permute-start.11 = (f32[2,64,128]{2,1,0:T(8,128)}, f32[2,64,128]{2,1,0:T(8,128)}, u32[]{:S(2)}, u32[]{:S(2)}) collective-permute-start(f32[2,64,128]{2,1,0:T(8,128)} %bitcast.74), channel_id=1, source_target_pairs={{0,32},{32,64},{64,96},{96,128},{128,160},{160,192},{192,224},{1,3... | collective-permute-start | bytes 196616 | tf_op jit(solution)/shard_map/ppermute | solution.py:19
  136.5 2.3 multiply_subtract_fusion.13
  142.0 2.3 multiply_subtract_fusion.14
  145.4 5.1 %collective-permute-start.14 = (f32[2,64,8]{1,2,0:T(8,128)S(1)}, f32[2,64,8]{1,2,0:T(8,128)S(1)}, u32[]{:S(2)}, u32[]{:S(2)}) collective-permute-start(f32[2,64,8]{1,2,0:T(8,128)S(1)} %pad_maximum_fusion.24), channel_id=1, source_target_pairs={{0,1},{1,2},{2,3},{3,4},{4,5},{5,6},{6,7},{7,8},{8,9},{9,10},{10,1... | collective-permute-start | bytes 12296 | tf_op jit(solution)/shard_map/ppermute | solution.py:19
  153.1 5.6 %collective-permute-start.15 = (f32[2,64,128]{2,1,0:T(8,128)}, f32[2,64,128]{2,1,0:T(8,128)}, u32[]{:S(2)}, u32[]{:S(2)}) collective-permute-start(f32[2,64,128]{2,1,0:T(8,128)} %fusion.12), channel_id=1, source_target_pairs={{0,32},{32,64},{64,96},{96,128},{128,160},{160,192},{192,224},{1,3... | collective-permute-start | bytes 196616 | tf_op jit(solution)/shard_map/ppermute | solution.py:19
  161.6 2.1 multiply_add_fusion.38
  181.4 2.4 multiply_subtract_fusion.11
  184.8 5.2 %collective-permute-start.18 = (f32[2,64,8]{1,2,0:T(8,128)S(1)}, f32[2,64,8]{1,2,0:T(8,128)S(1)}, u32[]{:S(2)}, u32[]{:S(2)}) collective-permute-start(f32[2,64,8]{1,2,0:T(8,128)S(1)} %pad_maximum_fusion.26), channel_id=1, source_target_pairs={{0,1},{1,2},{2,3},{3,4},{4,5},{5,6},{6,7},{7,8},{8,9},{9,10},{10,1... | collective-permute-start | bytes 12296 | tf_op jit(solution)/shard_map/ppermute | solution.py:19
  190.0 2.1 multiply_subtract_fusion.9
  192.9 4.5 collective-permute-start.19
  204.1 2.0 multiply_add_fusion.22
  217.3 2.1 multiply_subtract_fusion.7
  222.8 2.4 multiply_subtract_fusion.8
  226.9 4.8 %collective-permute-start.22 = (f32[2,64,8]{1,2,0:T(8,128)S(1)}, f32[2,64,8]{1,2,0:T(8,128)S(1)}, u32[]{:S(2)}, u32[]{:S(2)}) collective-permute-start(f32[2,64,8]{1,2,0:T(8,128)S(1)} %pad_maximum_fusion.28), channel_id=1, source_target_pairs={{0,1},{1,2},{2,3},{3,4},{4,5},{5,6},{6,7},{7,8},{8,9},{9,10},{10,1... | collective-permute-start | bytes 12296 | tf_op jit(solution)/shard_map/ppermute | solution.py:19
  234.4 5.8 %collective-permute-start.23 = (f32[2,64,128]{2,1,0:T(8,128)}, f32[2,64,128]{2,1,0:T(8,128)}, u32[]{:S(2)}, u32[]{:S(2)}) collective-permute-start(f32[2,64,128]{2,1,0:T(8,128)} %fusion.9), channel_id=1, source_target_pairs={{0,32},{32,64},{64,96},{96,128},{128,160},{160,192},{192,224},{1,3... | collective-permute-start | bytes 196616 | tf_op jit(solution)/shard_map/ppermute | solution.py:19
  266.4 5.9 %collective-permute-start.26 = (f32[2,64,8]{1,2,0:T(8,128)S(1)}, f32[2,64,8]{1,2,0:T(8,128)S(1)}, u32[]{:S(2)}, u32[]{:S(2)}) collective-permute-start(f32[2,64,8]{1,2,0:T(8,128)S(1)} %pad_maximum_fusion.30), channel_id=1, source_target_pairs={{0,1},{1,2},{2,3},{3,4},{4,5},{5,6},{6,7},{7,8},{8,9},{9,10},{10,1... | collective-permute-start | bytes 12296 | tf_op jit(solution)/shard_map/ppermute | solution.py:19
  272.4 2.1 multiply_subtract_fusion.3
  275.9 5.5 %collective-permute-start.27 = (f32[2,64,128]{2,1,0:T(8,128)}, f32[2,64,128]{2,1,0:T(8,128)}, u32[]{:S(2)}, u32[]{:S(2)}) collective-permute-start(f32[2,64,128]{2,1,0:T(8,128)} %fusion.8), channel_id=1, source_target_pairs={{0,32},{32,64},{64,96},{96,128},{128,160},{160,192},{192,224},{1,3... | collective-permute-start | bytes 196616 | tf_op jit(solution)/shard_map/ppermute | solution.py:19
  308.3 4.8 %collective-permute-start.30 = (f32[2,64,8]{1,2,0:T(8,128)S(1)}, f32[2,64,8]{1,2,0:T(8,128)S(1)}, u32[]{:S(2)}, u32[]{:S(2)}) collective-permute-start(f32[2,64,8]{1,2,0:T(8,128)S(1)} %pad_maximum_fusion.32), channel_id=1, source_target_pairs={{0,1},{1,2},{2,3},{3,4},{4,5},{5,6},{6,7},{7,8},{8,9},{9,10},{10,1... | collective-permute-start | bytes 12296 | tf_op jit(solution)/shard_map/ppermute | solution.py:19
  316.1 6.5 %collective-permute-start.31 = (f32[2,64,128]{2,1,0:T(8,128)S(1)}, f32[2,64,128]{2,1,0:T(8,128)}, u32[]{:S(2)}, u32[]{:S(2)}) collective-permute-start(f32[2,64,128]{2,1,0:T(8,128)S(1)} %bitcast.540), channel_id=1, source_target_pairs={{0,32},{32,64},{64,96},{96,128},{128,160},{160,192},{192,224},{1,3... | collective-permute-start | bytes 196616 | tf_op jit(solution)/shard_map/ppermute | solution.py:19
  322.8 2.0 constant_dynamic-update-slice_fusion.5
  331.2 2.1 gather_fusion
  334.6 9.6 %all-gather = f32[256,128]{1,0:T(8,128)S(1)} all-gather(f32[64,128]{1,0:T(8,128)S(1)} %fusion.1), channel_id=2, replica_groups=mesh['row_0'=4,'row_1'=2,'col_0'=8,'col_1'=2,'col_2'=2] {'row_0'}, dimensions={0}, use_global_device_ids=true | all-gather | bytes 163840 | tf_op jit(solution)/shard_map/all_gather | solution.py:24
  344.1 4.9 %all-gather.1 = f32[128,128]{1,0:T(8,128)S(1)} all-gather(f32[64,128]{1,0:T(8,128)S(1)} %reduce_sum.90), channel_id=3, replica_groups=mesh['row_0'=4,'row_1'=2,'col_0'=8,'col_1'=2,'col_2'=2] {'row_1'}, dimensions={0}, use_global_device_ids=true | all-gather | bytes 98304 | tf_op jit(solution)/shard_map/all_gather | solution.py:24
  349.1 28.6 %all-gather.2 = f32[512,128]{1,0:T(8,128)S(1)} all-gather(f32[64,128]{1,0:T(8,128)S(1)} %reduce_sum.91), channel_id=4, replica_groups=mesh['row_0'=4,'row_1'=2,'col_0'=8,'col_1'=2,'col_2'=2] {'col_0'}, dimensions={0}, use_global_device_ids=true | all-gather | bytes 294912 | tf_op jit(solution)/shard_map/all_gather | solution.py:24
  377.7 7.7 %all-gather.3 = f32[128,128]{1,0:T(8,128)S(1)} all-gather(f32[64,128]{1,0:T(8,128)S(1)} %reduce_sum.92), channel_id=5, replica_groups=mesh['row_0'=4,'row_1'=2,'col_0'=8,'col_1'=2,'col_2'=2] {'col_1'}, dimensions={0}, use_global_device_ids=true | all-gather | bytes 98304 | tf_op jit(solution)/shard_map/all_gather | solution.py:24
  385.5 13.9 %all-gather.4 = f32[128,128]{1,0:T(8,128)S(1)} all-gather(f32[64,128]{1,0:T(8,128)S(1)} %reduce_sum.93), channel_id=6, replica_groups=mesh['row_0'=4,'row_1'=2,'col_0'=8,'col_1'=2,'col_2'=2] {'col_2'}, dimensions={0}, use_global_device_ids=true | all-gather | bytes 98304 | tf_op jit(solution)/shard_map/all_gather | solution.py:24
  400.0 9.5 %all-gather.5 = f32[256,64]{1,0:T(8,128)S(1)} all-gather(f32[64,64]{1,0:T(8,128)S(1)} %fusion), channel_id=7, replica_groups=mesh['row_0'=4,'row_1'=2,'col_0'=8,'col_1'=2,'col_2'=2] {'row_0'}, dimensions={0}, use_global_device_ids=true | all-gather | bytes 81920 | tf_op jit(solution)/shard_map/all_gather | solution.py:24
  409.5 4.9 %all-gather.6 = f32[128,64]{1,0:T(8,128)S(1)} all-gather(f32[64,64]{1,0:T(8,128)S(1)} %reduce_sum.95), channel_id=8, replica_groups=mesh['row_0'=4,'row_1'=2,'col_0'=8,'col_1'=2,'col_2'=2] {'row_1'}, dimensions={0}, use_global_device_ids=true | all-gather | bytes 49152 | tf_op jit(solution)/shard_map/all_gather | solution.py:24
  414.5 19.0 %all-gather.7 = f32[512,64]{1,0:T(8,128)S(1)} all-gather(f32[64,64]{1,0:T(8,128)S(1)} %reduce_sum.96), channel_id=9, replica_groups=mesh['row_0'=4,'row_1'=2,'col_0'=8,'col_1'=2,'col_2'=2] {'col_0'}, dimensions={0}, use_global_device_ids=true | all-gather | bytes 147456 | tf_op jit(solution)/shard_map/all_gather | solution.py:24
  433.5 3.4 all-gather.8
  436.9 12.5 %all-gather.9 = f32[128,64]{1,0:T(8,128)S(1)} all-gather(f32[64,64]{1,0:T(8,128)S(1)} %reduce_sum.98), channel_id=11, replica_groups=mesh['row_0'=4,'row_1'=2,'col_0'=8,'col_1'=2,'col_2'=2] {'col_2'}, dimensions={0}, use_global_device_ids=true | all-gather | bytes 49152 | tf_op jit(solution)/shard_map/all_gather | solution.py:24
  (558 shorter events, 193.0 us)
Async XLA Ops:
  1.8 26.5 %collective-permute-start = (f32[2,64,128]{2,1,0:T(8,128)S(1)}, f32[2,64,128]{2,1,0:T(8,128)}, u32[]{:S(2)}, u32[]{:S(2)}) collective-permute-start(f32[2,64,128]{2,1,0:T(8,128)S(1)} %bitcast.542), channel_id=1, source_target_pairs={{32,0},{64,32},{96,64},{128,96},{160,128},{192,160},{224,192},{33,... | collective-permute-start | bytes 196616 | tf_op jit(solution)/shard_map/ppermute | solution.py:19
  4.1 12.9 %copy-start.1 = (f32[3,64,8,128]{3,2,1,0:T(8,128)S(1)}, f32[3,64,8,128]{3,2,1,0:T(8,128)}, u32[]{:S(2)}) copy-start(f32[3,64,8,128]{3,2,1,0:T(8,128)} %param.6) | copy-start | bytes 2359300
  4.5 22.6 %collective-permute-start.1 = (f32[2,64,8]{1,2,0:T(8,128)S(1)}, f32[2,64,8]{1,2,0:T(8,128)S(1)}, u32[]{:S(2)}, u32[]{:S(2)}) collective-permute-start(f32[2,64,8]{1,2,0:T(8,128)S(1)} %pad_maximum_fusion.17), channel_id=1, source_target_pairs={{1,0},{2,1},{3,2},{4,3},{5,4},{6,5},{7,6},{8,7},{9,8},{10,9},{11,1... | collective-permute-start | bytes 12296 | tf_op jit(solution)/shard_map/ppermute | solution.py:19
  10.7 14.9 %copy-start.109 = (s32[64]{0:T(128)S(1)}, s32[64]{0:T(128)}, u32[]{:S(2)}) copy-start(s32[64]{0:T(128)} %param.11) | copy-start | bytes 772
  10.7 148.0 %all-to-all-start = ((f32[16,64,128]{2,0,1:T(8,128)}), f32[16,64,128]{2,0,1:T(8,128)}, u32[]{:S(2)}, u32[]{:S(2)}) async-start(f32[16,64,128]{2,0,1:T(8,128)} %copy.1826), calls=%async_computation | async-start | bytes 1048576 | tf_op jit(solution)/shard_map/all_to_all | solution.py:126
  18.0 11.1 %copy-start.57 = (f32[3,64,8,128]{3,2,1,0:T(8,128)S(1)}, f32[3,64,8,128]{3,2,1,0:T(8,128)}, u32[]{:S(2)}) copy-start(f32[3,64,8,128]{3,2,1,0:T(8,128)} %param.7) | copy-start | bytes 2359300
  20.6 10.6 %copy-start.95 = (f32[128]{0:T(128)}, f32[128]{0:T(128)S(1)}, u32[]{:S(2)}) copy-start(f32[128]{0:T(128)S(1)} %get-tuple-element.93) | copy-start | bytes 1540
  21.9 26.0 %copy-start.98 = (f32[128]{0:T(128)}, f32[128]{0:T(128)S(1)}, u32[]{:S(2)}) copy-start(f32[128]{0:T(128)S(1)} %get-tuple-element.82) | copy-start | bytes 1540
  23.8 13.1 %copy-start.101 = (f32[8]{0:T(128)}, f32[8]{0:T(128)S(1)}, u32[]{:S(2)}) copy-start(f32[8]{0:T(128)S(1)} %get-tuple-element.88) | copy-start | bytes 100
  26.4 21.5 %copy-start.68 = (f32[8]{0:T(128)}, f32[8]{0:T(128)S(1)}, u32[]{:S(2)}) copy-start(f32[8]{0:T(128)S(1)} %fusion.20) | copy-start | bytes 100
  33.3 31.9 %copy-start.6 = (f32[64,8,128]{2,1,0:T(8,128)}, f32[64,8,128]{2,1,0:T(8,128)S(1)}, u32[]{:S(2)}) copy-start(f32[64,8,128]{2,1,0:T(8,128)S(1)} %get-tuple-element.92) | copy-start | bytes 786436
  33.6 12.0 %collective-permute-start.2 = (f32[2,64,8]{1,2,0:T(8,128)S(1)}, f32[2,64,8]{1,2,0:T(8,128)S(1)}, u32[]{:S(2)}, u32[]{:S(2)}) collective-permute-start(f32[2,64,8]{1,2,0:T(8,128)S(1)} %pad_maximum_fusion.18), channel_id=1, source_target_pairs={{0,1},{1,2},{2,3},{3,4},{4,5},{5,6},{6,7},{7,8},{8,9},{9,10},{10,1... | collective-permute-start | bytes 12296 | tf_op jit(solution)/shard_map/ppermute | solution.py:19
  39.8 8.0 %collective-permute-start.3 = (f32[2,64,128]{2,1,0:T(8,128)S(1)}, f32[2,64,128]{2,1,0:T(8,128)S(1)}, u32[]{:S(2)}, u32[]{:S(2)}) collective-permute-start(f32[2,64,128]{2,1,0:T(8,128)S(1)} %bitcast.539), channel_id=1, source_target_pairs={{0,32},{32,64},{64,96},{96,128},{128,160},{160,192},{192,224},{1,3... | collective-permute-start | bytes 196616 | tf_op jit(solution)/shard_map/ppermute | solution.py:19
  50.2 7.0 %collective-permute-start.5 = (f32[2,64,8]{1,2,0:T(8,128)S(1)}, f32[2,64,8]{1,2,0:T(8,128)S(1)}, u32[]{:S(2)}, u32[]{:S(2)}) collective-permute-start(f32[2,64,8]{1,2,0:T(8,128)S(1)} %pad_maximum_fusion.19), channel_id=1, source_target_pairs={{1,0},{2,1},{3,2},{4,3},{5,4},{6,5},{7,6},{8,7},{9,8},{10,9},{11,1... | collective-permute-start | bytes 12296 | tf_op jit(solution)/shard_map/ppermute | solution.py:19
  55.8 6.7 %collective-permute-start.4 = (f32[2,64,128]{2,1,0:T(8,128)}, f32[2,64,128]{2,1,0:T(8,128)S(1)}, u32[]{:S(2)}, u32[]{:S(2)}) collective-permute-start(f32[2,64,128]{2,1,0:T(8,128)} %fusion.16), channel_id=1, source_target_pairs={{32,0},{64,32},{96,64},{128,96},{160,128},{192,160},{224,192},{33,... | collective-permute-start | bytes 196616 | tf_op jit(solution)/shard_map/ppermute | solution.py:19
  67.5 12.6 %copy-start.76 = (f32[128]{0:T(128)S(1)}, f32[128]{0:T(128)}, u32[]{:S(2)}) copy-start(f32[128]{0:T(128)} %copy-done.75) | copy-start | bytes 1540
  67.5 12.6 %copy-start.99 = (f32[128]{0:T(128)S(1)}, f32[128]{0:T(128)}, u32[]{:S(2)}) copy-start(f32[128]{0:T(128)} %copy-done.98) | copy-start | bytes 1540
  67.8 12.2 %collective-permute-start.6 = (f32[2,64,8]{1,2,0:T(8,128)S(1)}, f32[2,64,8]{1,2,0:T(8,128)S(1)}, u32[]{:S(2)}, u32[]{:S(2)}) collective-permute-start(f32[2,64,8]{1,2,0:T(8,128)S(1)} %pad_maximum_fusion.20), channel_id=1, source_target_pairs={{0,1},{1,2},{2,3},{3,4},{4,5},{5,6},{6,7},{7,8},{8,9},{9,10},{10,1... | collective-permute-start | bytes 12296 | tf_op jit(solution)/shard_map/ppermute | solution.py:19
  74.1 10.2 %collective-permute-start.7 = (f32[2,64,128]{2,1,0:T(8,128)}, f32[2,64,128]{2,1,0:T(8,128)}, u32[]{:S(2)}, u32[]{:S(2)}) collective-permute-start(f32[2,64,128]{2,1,0:T(8,128)} %fusion.15), channel_id=1, source_target_pairs={{0,32},{32,64},{64,96},{96,128},{128,160},{160,192},{192,224},{1,3... | collective-permute-start | bytes 196616 | tf_op jit(solution)/shard_map/ppermute | solution.py:19
  87.9 6.9 %collective-permute-start.9 = (f32[2,64,8]{1,2,0:T(8,128)S(1)}, f32[2,64,8]{1,2,0:T(8,128)S(1)}, u32[]{:S(2)}, u32[]{:S(2)}) collective-permute-start(f32[2,64,8]{1,2,0:T(8,128)S(1)} %pad_maximum_fusion.21), channel_id=1, source_target_pairs={{1,0},{2,1},{3,2},{4,3},{5,4},{6,5},{7,6},{8,7},{9,8},{10,9},{11,1... | collective-permute-start | bytes 12296 | tf_op jit(solution)/shard_map/ppermute | solution.py:19
  93.5 6.8 %collective-permute-start.8 = (f32[2,64,128]{2,1,0:T(8,128)}, f32[2,64,128]{2,1,0:T(8,128)}, u32[]{:S(2)}, u32[]{:S(2)}) collective-permute-start(f32[2,64,128]{2,1,0:T(8,128)} %fusion.14), channel_id=1, source_target_pairs={{32,0},{64,32},{96,64},{128,96},{160,128},{192,160},{224,192},{33,... | collective-permute-start | bytes 196616 | tf_op jit(solution)/shard_map/ppermute | solution.py:19
  104.4 13.5 %collective-permute-start.10 = (f32[2,64,8]{1,2,0:T(8,128)S(1)}, f32[2,64,8]{1,2,0:T(8,128)S(1)}, u32[]{:S(2)}, u32[]{:S(2)}) collective-permute-start(f32[2,64,8]{1,2,0:T(8,128)S(1)} %pad_maximum_fusion.22), channel_id=1, source_target_pairs={{0,1},{1,2},{2,3},{3,4},{4,5},{5,6},{6,7},{7,8},{8,9},{9,10},{10,1... | collective-permute-start | bytes 12296 | tf_op jit(solution)/shard_map/ppermute | solution.py:19
  113.0 9.7 %collective-permute-start.11 = (f32[2,64,128]{2,1,0:T(8,128)}, f32[2,64,128]{2,1,0:T(8,128)}, u32[]{:S(2)}, u32[]{:S(2)}) collective-permute-start(f32[2,64,128]{2,1,0:T(8,128)} %bitcast.74), channel_id=1, source_target_pairs={{0,32},{32,64},{64,96},{96,128},{128,160},{160,192},{192,224},{1,3... | collective-permute-start | bytes 196616 | tf_op jit(solution)/shard_map/ppermute | solution.py:19
  125.0 42.0 %copy-start.13 = (f32[64,8,128]{2,1,0:T(8,128)}, f32[64,8,128]{2,1,0:T(8,128)S(1)}, u32[]{:S(2)}) copy-start(f32[64,8,128]{2,1,0:T(8,128)S(1)} %get-tuple-element.59) | copy-start | bytes 786436
  127.7 7.8 %collective-permute-start.13 = (f32[2,64,8]{1,2,0:T(8,128)S(1)}, f32[2,64,8]{1,2,0:T(8,128)S(1)}, u32[]{:S(2)}, u32[]{:S(2)}) collective-permute-start(f32[2,64,8]{1,2,0:T(8,128)S(1)} %pad_maximum_fusion.23), channel_id=1, source_target_pairs={{1,0},{2,1},{3,2},{4,3},{5,4},{6,5},{7,6},{8,7},{9,8},{10,9},{11,1... | collective-permute-start | bytes 12296 | tf_op jit(solution)/shard_map/ppermute | solution.py:19
  134.1 7.1 %collective-permute-start.12 = (f32[2,64,128]{2,1,0:T(8,128)}, f32[2,64,128]{2,1,0:T(8,128)}, u32[]{:S(2)}, u32[]{:S(2)}) collective-permute-start(f32[2,64,128]{2,1,0:T(8,128)} %fusion.13), channel_id=1, source_target_pairs={{32,0},{64,32},{96,64},{128,96},{160,128},{192,160},{224,192},{33,... | collective-permute-start | bytes 196616 | tf_op jit(solution)/shard_map/ppermute | solution.py:19
  145.4 15.3 %collective-permute-start.14 = (f32[2,64,8]{1,2,0:T(8,128)S(1)}, f32[2,64,8]{1,2,0:T(8,128)S(1)}, u32[]{:S(2)}, u32[]{:S(2)}) collective-permute-start(f32[2,64,8]{1,2,0:T(8,128)S(1)} %pad_maximum_fusion.24), channel_id=1, source_target_pairs={{0,1},{1,2},{2,3},{3,4},{4,5},{5,6},{6,7},{7,8},{8,9},{9,10},{10,1... | collective-permute-start | bytes 12296 | tf_op jit(solution)/shard_map/ppermute | solution.py:19
  151.7 9.9 %copy-start.38 = (f32[64,8,1]{2,1,0:T(8,128)S(1)}, f32[64,8,1]{2,1,0:T(8,128)}, u32[]{:S(2)}) copy-start(f32[64,8,1]{2,1,0:T(8,128)} %copy-done.37) | copy-start | bytes 6148
  151.7 9.9 %copy-start.77 = (f32[128]{0:T(128)S(1)}, f32[128]{0:T(128)}, u32[]{:S(2)}) copy-start(f32[128]{0:T(128)} %copy-done.75) | copy-start | bytes 1540
  153.1 13.1 %collective-permute-start.15 = (f32[2,64,128]{2,1,0:T(8,128)}, f32[2,64,128]{2,1,0:T(8,128)}, u32[]{:S(2)}, u32[]{:S(2)}) collective-permute-start(f32[2,64,128]{2,1,0:T(8,128)} %fusion.12), channel_id=1, source_target_pairs={{0,32},{32,64},{64,96},{96,128},{128,160},{160,192},{192,224},{1,3... | collective-permute-start | bytes 196616 | tf_op jit(solution)/shard_map/ppermute | solution.py:19
  169.5 5.5 %collective-permute-start.17 = (f32[2,64,8]{1,2,0:T(8,128)S(1)}, f32[2,64,8]{1,2,0:T(8,128)S(1)}, u32[]{:S(2)}, u32[]{:S(2)}) collective-permute-start(f32[2,64,8]{1,2,0:T(8,128)S(1)} %pad_maximum_fusion.25), channel_id=1, source_target_pairs={{1,0},{2,1},{3,2},{4,3},{5,4},{6,5},{7,6},{8,7},{9,8},{10,9},{11,1... | collective-permute-start | bytes 12296 | tf_op jit(solution)/shard_map/ppermute | solution.py:19
  173.7 6.9 %collective-permute-start.16 = (f32[2,64,128]{2,1,0:T(8,128)}, f32[2,64,128]{2,1,0:T(8,128)}, u32[]{:S(2)}, u32[]{:S(2)}) collective-permute-start(f32[2,64,128]{2,1,0:T(8,128)} %fusion.11), channel_id=1, source_target_pairs={{32,0},{64,32},{96,64},{128,96},{160,128},{192,160},{224,192},{33,... | collective-permute-start | bytes 196616 | tf_op jit(solution)/shard_map/ppermute | solution.py:19
  184.8 12.5 %collective-permute-start.18 = (f32[2,64,8]{1,2,0:T(8,128)S(1)}, f32[2,64,8]{1,2,0:T(8,128)S(1)}, u32[]{:S(2)}, u32[]{:S(2)}) collective-permute-start(f32[2,64,8]{1,2,0:T(8,128)S(1)} %pad_maximum_fusion.26), channel_id=1, source_target_pairs={{0,1},{1,2},{2,3},{3,4},{4,5},{5,6},{6,7},{7,8},{8,9},{9,10},{10,1... | collective-permute-start | bytes 12296 | tf_op jit(solution)/shard_map/ppermute | solution.py:19
  192.9 10.4 %collective-permute-start.19 = (f32[2,64,128]{2,1,0:T(8,128)S(1)}, f32[2,64,128]{2,1,0:T(8,128)}, u32[]{:S(2)}, u32[]{:S(2)}) collective-permute-start(f32[2,64,128]{2,1,0:T(8,128)S(1)} %bitcast.541), channel_id=1, source_target_pairs={{0,32},{32,64},{64,96},{96,128},{128,160},{160,192},{192,224},{1,3... | collective-permute-start | bytes 196616 | tf_op jit(solution)/shard_map/ppermute | solution.py:19
  208.8 7.6 %collective-permute-start.21 = (f32[2,64,8]{1,2,0:T(8,128)S(1)}, f32[2,64,8]{1,2,0:T(8,128)S(1)}, u32[]{:S(2)}, u32[]{:S(2)}) collective-permute-start(f32[2,64,8]{1,2,0:T(8,128)S(1)} %pad_maximum_fusion.27), channel_id=1, source_target_pairs={{1,0},{2,1},{3,2},{4,3},{5,4},{6,5},{7,6},{8,7},{9,8},{10,9},{11,1... | collective-permute-start | bytes 12296 | tf_op jit(solution)/shard_map/ppermute | solution.py:19
  215.1 6.8 %collective-permute-start.20 = (f32[2,64,128]{2,1,0:T(8,128)}, f32[2,64,128]{2,1,0:T(8,128)}, u32[]{:S(2)}, u32[]{:S(2)}) collective-permute-start(f32[2,64,128]{2,1,0:T(8,128)} %fusion.10), channel_id=1, source_target_pairs={{32,0},{64,32},{96,64},{128,96},{160,128},{192,160},{224,192},{33,... | collective-permute-start | bytes 196616 | tf_op jit(solution)/shard_map/ppermute | solution.py:19
  226.9 13.3 %collective-permute-start.22 = (f32[2,64,8]{1,2,0:T(8,128)S(1)}, f32[2,64,8]{1,2,0:T(8,128)S(1)}, u32[]{:S(2)}, u32[]{:S(2)}) collective-permute-start(f32[2,64,8]{1,2,0:T(8,128)S(1)} %pad_maximum_fusion.28), channel_id=1, source_target_pairs={{0,1},{1,2},{2,3},{3,4},{4,5},{5,6},{6,7},{7,8},{8,9},{9,10},{10,1... | collective-permute-start | bytes 12296 | tf_op jit(solution)/shard_map/ppermute | solution.py:19
  234.4 10.4 %collective-permute-start.23 = (f32[2,64,128]{2,1,0:T(8,128)}, f32[2,64,128]{2,1,0:T(8,128)}, u32[]{:S(2)}, u32[]{:S(2)}) collective-permute-start(f32[2,64,128]{2,1,0:T(8,128)} %fusion.9), channel_id=1, source_target_pairs={{0,32},{32,64},{64,96},{96,128},{128,160},{160,192},{192,224},{1,3... | collective-permute-start | bytes 196616 | tf_op jit(solution)/shard_map/ppermute | solution.py:19
  248.2 8.0 %collective-permute-start.25 = (f32[2,64,8]{1,2,0:T(8,128)S(1)}, f32[2,64,8]{1,2,0:T(8,128)S(1)}, u32[]{:S(2)}, u32[]{:S(2)}) collective-permute-start(f32[2,64,8]{1,2,0:T(8,128)S(1)} %pad_maximum_fusion.29), channel_id=1, source_target_pairs={{1,0},{2,1},{3,2},{4,3},{5,4},{6,5},{7,6},{8,7},{9,8},{10,9},{11,1... | collective-permute-start | bytes 12296 | tf_op jit(solution)/shard_map/ppermute | solution.py:19
  255.0 6.8 %collective-permute-start.24 = (f32[2,64,128]{2,1,0:T(8,128)}, f32[2,64,128]{2,1,0:T(8,128)}, u32[]{:S(2)}, u32[]{:S(2)}) collective-permute-start(f32[2,64,128]{2,1,0:T(8,128)} %bitcast.148), channel_id=1, source_target_pairs={{32,0},{64,32},{96,64},{128,96},{160,128},{192,160},{224,192},{33,... | collective-permute-start | bytes 196616 | tf_op jit(solution)/shard_map/ppermute | solution.py:19
  266.4 15.0 %collective-permute-start.26 = (f32[2,64,8]{1,2,0:T(8,128)S(1)}, f32[2,64,8]{1,2,0:T(8,128)S(1)}, u32[]{:S(2)}, u32[]{:S(2)}) collective-permute-start(f32[2,64,8]{1,2,0:T(8,128)S(1)} %pad_maximum_fusion.30), channel_id=1, source_target_pairs={{0,1},{1,2},{2,3},{3,4},{4,5},{5,6},{6,7},{7,8},{8,9},{9,10},{10,1... | collective-permute-start | bytes 12296 | tf_op jit(solution)/shard_map/ppermute | solution.py:19
  275.9 10.9 %collective-permute-start.27 = (f32[2,64,128]{2,1,0:T(8,128)}, f32[2,64,128]{2,1,0:T(8,128)}, u32[]{:S(2)}, u32[]{:S(2)}) collective-permute-start(f32[2,64,128]{2,1,0:T(8,128)} %fusion.8), channel_id=1, source_target_pairs={{0,32},{32,64},{64,96},{96,128},{128,160},{160,192},{192,224},{1,3... | collective-permute-start | bytes 196616 | tf_op jit(solution)/shard_map/ppermute | solution.py:19
  291.5 7.7 %collective-permute-start.29 = (f32[2,64,8]{1,2,0:T(8,128)S(1)}, f32[2,64,8]{1,2,0:T(8,128)S(1)}, u32[]{:S(2)}, u32[]{:S(2)}) collective-permute-start(f32[2,64,8]{1,2,0:T(8,128)S(1)} %pad_maximum_fusion.31), channel_id=1, source_target_pairs={{1,0},{2,1},{3,2},{4,3},{5,4},{6,5},{7,6},{8,7},{9,8},{10,9},{11,1... | collective-permute-start | bytes 12296 | tf_op jit(solution)/shard_map/ppermute | solution.py:19
  297.9 6.8 %collective-permute-start.28 = (f32[2,64,128]{2,1,0:T(8,128)}, f32[2,64,128]{2,1,0:T(8,128)}, u32[]{:S(2)}, u32[]{:S(2)}) collective-permute-start(f32[2,64,128]{2,1,0:T(8,128)} %fusion.7), channel_id=1, source_target_pairs={{32,0},{64,32},{96,64},{128,96},{160,128},{192,160},{224,192},{33,... | collective-permute-start | bytes 196616 | tf_op jit(solution)/shard_map/ppermute | solution.py:19
  308.3 14.3 %collective-permute-start.30 = (f32[2,64,8]{1,2,0:T(8,128)S(1)}, f32[2,64,8]{1,2,0:T(8,128)S(1)}, u32[]{:S(2)}, u32[]{:S(2)}) collective-permute-start(f32[2,64,8]{1,2,0:T(8,128)S(1)} %pad_maximum_fusion.32), channel_id=1, source_target_pairs={{0,1},{1,2},{2,3},{3,4},{4,5},{5,6},{6,7},{7,8},{8,9},{9,10},{10,1... | collective-permute-start | bytes 12296 | tf_op jit(solution)/shard_map/ppermute | solution.py:19
  316.1 8.9 %collective-permute-start.31 = (f32[2,64,128]{2,1,0:T(8,128)S(1)}, f32[2,64,128]{2,1,0:T(8,128)}, u32[]{:S(2)}, u32[]{:S(2)}) collective-permute-start(f32[2,64,128]{2,1,0:T(8,128)S(1)} %bitcast.540), channel_id=1, source_target_pairs={{0,32},{32,64},{64,96},{96,128},{128,160},{160,192},{192,224},{1,3... | collective-permute-start | bytes 196616 | tf_op jit(solution)/shard_map/ppermute | solution.py:19
  334.5 115.5 %copy-start.58 = (f32[1,64,8,128]{3,2,1,0:T(8,128)S(1)}, f32[1,64,8,128]{3,2,1,0:T(8,128)}, u32[]{:S(2)}) copy-start(f32[1,64,8,128]{3,2,1,0:T(8,128)} %get-tuple-element.25) | copy-start | bytes 786436
  334.5 115.5 %copy-start.59 = (f32[1,64,8,128]{3,2,1,0:T(8,128)S(1)}, f32[1,64,8,128]{3,2,1,0:T(8,128)}, u32[]{:S(2)}) copy-start(f32[1,64,8,128]{3,2,1,0:T(8,128)} %get-tuple-element.23) | copy-start | bytes 786436
  (95 other events, 484.2 us)
